TPU v7x, 32 devices: a whole 2x2x4 slice. The times are simulated.
32 devices in a mesh: replica: 2 (over x), fsdp: 16 (over z, y, core).
Axes of the slice: x: 2, y: 2, z: 4, core: 2. Of those that a mesh axis runs over, the one named last changes fastest.
Arguments:
- tokens: bfloat16 [16384, 768], P(('replica', 'fsdp')), may hold values from -6 to 6
- cotangent: bfloat16 [16384, 768], P(('replica', 'fsdp')), may hold values from -6 to 6
- qkv_weight: bfloat16 [768, 2304], P('fsdp'), may hold values from -0.21875 to 0.21875
- qkv_bias: bfloat16 [2304], P('fsdp'), may hold values from -3 to 3
- proj_weight: bfloat16 [768, 768], P('fsdp'), may hold values from -1.75 to 1.75
- proj_bias: bfloat16 [768], P('fsdp'), may hold values from -3 to 3
- attn_gain: bfloat16 [768], P('fsdp'), may hold values from 0.5 to 1.5
- attn_shift: bfloat16 [768], P('fsdp'), may hold values from -3 to 3
- inner_weight: bfloat16 [768, 3072], P('fsdp'), may hold values from -0.21875 to 0.21875
- inner_bias: bfloat16 [3072], P('fsdp'), may hold values from -3 to 3
- outer_weight: bfloat16 [3072, 768], P('fsdp'), may hold values from -0.21875 to 0.21875
- outer_bias: bfloat16 [768], P('fsdp'), may hold values from -3 to 3
- ffn_gain: bfloat16 [768], P('fsdp'), may hold values from 0.5 to 1.5
- ffn_shift: bfloat16 [768], P('fsdp'), may hold values from -3 to 3
- random_dirs: bfloat16 [12, 64, 256], replicated, may hold values from -5 to 5
- seq_lengths: int32 [2, 16, 4], P('replica', 'fsdp'), may hold values from 1 to 256, 448 in all within a row
- deal_order: int32 [2, 16], P('replica'), may hold values from 0 to 15, each once within a row
Outputs:
- layer_out: bfloat16 [16384, 768], P(('replica', 'fsdp'))
- tokens_grad: bfloat16 [16384, 768], P(('replica', 'fsdp'))
- qkv_weight_grad: float32 [768, 2304], P('fsdp')
- qkv_bias_grad: float32 [2304], P('fsdp')
- proj_weight_grad: float32 [768, 768], P('fsdp')
- proj_bias_grad: float32 [768], P('fsdp')
- attn_gain_grad: float32 [768], P('fsdp')
- attn_shift_grad: float32 [768], P('fsdp')
- inner_weight_grad: float32 [768, 3072], P('fsdp')
- inner_bias_grad: float32 [3072], P('fsdp')
- outer_weight_grad: float32 [3072, 768], P('fsdp')
- outer_bias_grad: float32 [768], P('fsdp')
- ffn_gain_grad: float32 [768], P('fsdp')
- ffn_shift_grad: float32 [768], P('fsdp')
Inputs may be any that keep to these rules, and one draw needn't show every extreme that they name: `seq_lengths`: the 4 sequences of each dealt buffer lie one after another in its first 448 rows, the longest of each exactly 256 rows; the last 64 rows are padding. `deal_order`: each row is a permutation of the 16 buffers of one replica group.
All inputs are finite; a program needn't handle non-finite values.
Results may differ from a plain program's by a relative error of at most 0.03.
Values may be sent and summed in bfloat16 or wider, within the bound.
A program may use at most 128 MiB of HBM per device.

v0:
```python
from functools import partial
import jax
import jax.numpy as jnp
from jax import lax
from jax.sharding import PartitionSpec as P

EPSILON = 1e-06


def layer_norm(summed, gain_vec, shift_vec):
    centered = summed - jnp.mean(summed, -1, keepdims=True)
    inv_std = lax.rsqrt(jnp.mean(centered * centered, -1, keepdims=True) + EPSILON)
    return centered * inv_std * gain_vec + shift_vec


def matrix_product(left, right):
    return jnp.dot(left, right, preferred_element_type=jnp.float32)


def rows_product(left, right):
    return lax.dot_general(
        left, right, (((0,), (0,)), ((), ())), preferred_element_type=jnp.float32
    )


def back_product(left, right):
    return lax.dot_general(
        left, right, (((1,), (1,)), ((), ())), preferred_element_type=jnp.float32
    )


def feature_map(scaled, directions):
    project = jnp.einsum("rhd,hdm->rhm", scaled, directions, preferred_element_type=jnp.float32)
    widened = scaled.astype(jnp.float32)
    return jnp.exp(project - 0.5 * jnp.sum(widened * widened, -1, keepdims=True))


def feature_back(dfeature, feature, scaled, directions):
    dexponent = dfeature * feature
    dproject = dexponent.astype(jnp.bfloat16)
    dscaled = jnp.einsum("rhm,hdm->rhd", dproject, directions, preferred_element_type=jnp.float32)
    return dscaled - scaled.astype(jnp.float32) * jnp.sum(dexponent, -1, keepdims=True)


def unpack(gathered):
    return tuple(
        (tensor.astype(jnp.float32) if tensor.ndim == 1 else tensor for tensor in gathered)
    )


def column_sum(values_low):
    return jnp.sum(values_low.astype(jnp.float32), axis=0)


def body(
    tokens,
    cotangent,
    qkv_weight,
    qkv_bias,
    proj_weight,
    proj_bias,
    attn_gain,
    attn_shift,
    inner_weight,
    inner_bias,
    outer_weight,
    outer_bias,
    ffn_gain,
    ffn_shift,
    random_dirs,
    seq_lengths,
    deal_order,
):
    groups = lax.axis_size("fsdp")
    row_count, model_width = tokens.shape
    piece_rows = row_count // groups
    deal_row = deal_order[0]
    send_tokens = jnp.take(tokens.reshape(groups, piece_rows, model_width), deal_row, axis=0)
    send_grads = jnp.take(cotangent.reshape(groups, piece_rows, model_width), deal_row, axis=0)
    arrived_x, arrived_g = (
        lax.all_to_all(send_tokens, "fsdp", split_axis=0, concat_axis=0, tiled=True),
        lax.all_to_all(send_grads, "fsdp", split_axis=0, concat_axis=0, tiled=True),
    )
    token_low = arrived_x.reshape(row_count, model_width)
    upstream = arrived_g.reshape(row_count, model_width).astype(jnp.float32)
    gathered = (
        lax.all_gather(qkv_weight, "fsdp", axis=0, tiled=True),
        lax.all_gather(qkv_bias, "fsdp", axis=0, tiled=True),
        lax.all_gather(proj_weight, "fsdp", axis=0, tiled=True),
        lax.all_gather(proj_bias, "fsdp", axis=0, tiled=True),
        lax.all_gather(attn_gain, "fsdp", axis=0, tiled=True),
        lax.all_gather(attn_shift, "fsdp", axis=0, tiled=True),
        lax.all_gather(inner_weight, "fsdp", axis=0, tiled=True),
        lax.all_gather(inner_bias, "fsdp", axis=0, tiled=True),
        lax.all_gather(outer_weight, "fsdp", axis=0, tiled=True),
        lax.all_gather(outer_bias, "fsdp", axis=0, tiled=True),
        lax.all_gather(ffn_gain, "fsdp", axis=0, tiled=True),
        lax.all_gather(ffn_shift, "fsdp", axis=0, tiled=True),
    )
    (
        weight_qkv,
        bias_qkv,
        weight_proj,
        bias_proj,
        gain_attn,
        shift_attn,
        weight_inner,
        bias_inner,
        weight_outer,
        bias_outer,
        gain_ffn,
        shift_ffn,
    ) = unpack(gathered)
    lengths_here = seq_lengths[0, 0]
    seq_ends = jnp.cumsum(lengths_here)
    slot_count = lengths_here.shape[0] + 1
    position = lax.iota(jnp.int32, row_count)
    segment = jnp.sum((position[:, None] >= seq_ends[None, :]).astype(jnp.int32), axis=1)
    select_low = (segment[:, None] == lax.iota(jnp.int32, slot_count)[None, :]).astype(jnp.bfloat16)
    valid_rows = (segment < slot_count - 1).astype(jnp.float32)[:, None]
    head_count, head_dim = (random_dirs.shape[0], random_dirs.shape[1])
    feature_scale = head_dim ** (-0.25)
    qkv_act = matrix_product(token_low, weight_qkv) + bias_qkv
    query_act, key_act, value_act = jnp.split(qkv_act, 3, axis=1)
    query_low = (
        (query_act * feature_scale).astype(jnp.bfloat16).reshape(row_count, head_count, head_dim)
    )
    key_low = (
        (key_act * feature_scale).astype(jnp.bfloat16).reshape(row_count, head_count, head_dim)
    )
    value_low = value_act.astype(jnp.bfloat16).reshape(row_count, head_count, head_dim)
    query_feat = feature_map(query_low, random_dirs)
    key_feat = feature_map(key_low, random_dirs)
    qfeat_low = query_feat.astype(jnp.bfloat16)
    kfeat_low = key_feat.astype(jnp.bfloat16)
    masked_keys = select_low[:, :, None, None] * kfeat_low[:, None]
    masked_query = select_low[:, :, None, None] * qfeat_low[:, None]
    kv_state = jnp.einsum(
        "rshm,rhe->shme", masked_keys, value_low, preferred_element_type=jnp.float32
    ).astype(jnp.bfloat16)
    key_total = jnp.einsum(
        "rs,rhm->shm", select_low, kfeat_low, preferred_element_type=jnp.float32
    ).astype(jnp.bfloat16)
    numerator = jnp.einsum(
        "rshm,shme->rhe", masked_query, kv_state, preferred_element_type=jnp.float32
    )
    denominator = jnp.einsum(
        "rshm,shm->rh", masked_query, key_total, preferred_element_type=jnp.float32
    )
    context_low = (
        (numerator / denominator[:, :, None]).reshape(row_count, model_width).astype(jnp.bfloat16)
    )
    attn_out = matrix_product(context_low, weight_proj) + bias_proj
    hidden, first_pull = jax.vjp(
        layer_norm, token_low.astype(jnp.float32) + attn_out, gain_attn, shift_attn
    )
    hidden_low = hidden.astype(jnp.bfloat16)
    inner_act = matrix_product(hidden_low, weight_inner) + bias_inner
    gelu_act, gelu_pull = jax.vjp(partial(jax.nn.gelu, approximate=False), inner_act)
    gelu_low = gelu_act.astype(jnp.bfloat16)
    outer_act = matrix_product(gelu_low, weight_outer) + bias_outer
    normed_out, second_pull = jax.vjp(layer_norm, hidden + outer_act, gain_ffn, shift_ffn)
    result = normed_out * valid_rows
    regathered = (
        lax.all_gather(qkv_weight, "fsdp", axis=0, tiled=True),
        lax.all_gather(qkv_bias, "fsdp", axis=0, tiled=True),
        lax.all_gather(proj_weight, "fsdp", axis=0, tiled=True),
        lax.all_gather(proj_bias, "fsdp", axis=0, tiled=True),
        lax.all_gather(attn_gain, "fsdp", axis=0, tiled=True),
        lax.all_gather(attn_shift, "fsdp", axis=0, tiled=True),
        lax.all_gather(inner_weight, "fsdp", axis=0, tiled=True),
        lax.all_gather(inner_bias, "fsdp", axis=0, tiled=True),
        lax.all_gather(outer_weight, "fsdp", axis=0, tiled=True),
        lax.all_gather(outer_bias, "fsdp", axis=0, tiled=True),
        lax.all_gather(ffn_gain, "fsdp", axis=0, tiled=True),
        lax.all_gather(ffn_shift, "fsdp", axis=0, tiled=True),
    )
    back_weights = unpack(regathered)
    back_qkv = back_weights[0]
    back_proj = back_weights[2]
    back_inner = back_weights[6]
    back_outer = back_weights[8]
    dsecond, grad_gain_ffn, grad_shift_ffn = second_pull(upstream * valid_rows)
    douter_low = dsecond.astype(jnp.bfloat16)
    grad_bias_outer = column_sum(douter_low)
    grad_weight_outer = rows_product(gelu_low, douter_low)
    dinner_low = gelu_pull(back_product(douter_low, back_outer))[0].astype(jnp.bfloat16)
    grad_bias_inner = column_sum(dinner_low)
    grad_weight_inner = rows_product(hidden_low, dinner_low)
    dhidden = dsecond + back_product(dinner_low, back_inner)
    dfirst, grad_gain_attn, grad_shift_attn = first_pull(dhidden)
    dattn_low = dfirst.astype(jnp.bfloat16)
    grad_bias_proj = column_sum(dattn_low)
    grad_weight_proj = rows_product(context_low, dattn_low)
    dcontext = back_product(dattn_low, back_proj).reshape(row_count, head_count, head_dim)
    dnumer_low = (dcontext / denominator[:, :, None]).astype(jnp.bfloat16)
    ddenom_low = (-jnp.sum(dcontext * numerator, -1) / jnp.square(denominator)).astype(jnp.bfloat16)
    masked_dnumer = select_low[:, :, None, None] * dnumer_low[:, None]
    key_rows = jnp.einsum("rs,shm->rhm", select_low, key_total, preferred_element_type=jnp.float32)
    dqfeat = jnp.einsum(
        "rshe,shme->rhm", masked_dnumer, kv_state, preferred_element_type=jnp.float32
    )
    dqfeat = dqfeat + ddenom_low.astype(jnp.float32)[:, :, None] * key_rows
    dstate_low = jnp.einsum(
        "rshm,rhe->shme", masked_query, dnumer_low, preferred_element_type=jnp.float32
    ).astype(jnp.bfloat16)
    dtotal_low = jnp.einsum(
        "rshm,rh->shm", masked_query, ddenom_low, preferred_element_type=jnp.float32
    ).astype(jnp.bfloat16)
    masked_values = select_low[:, :, None, None] * value_low[:, None]
    dkfeat = jnp.einsum(
        "rshe,shme->rhm", masked_values, dstate_low, preferred_element_type=jnp.float32
    )
    dkfeat = dkfeat + jnp.einsum(
        "rs,shm->rhm", select_low, dtotal_low, preferred_element_type=jnp.float32
    )
    dvalues = jnp.einsum(
        "rshm,shme->rhe", masked_keys, dstate_low, preferred_element_type=jnp.float32
    )
    dquery = feature_back(dqfeat, query_feat, query_low, random_dirs) * feature_scale
    dkeys = feature_back(dkfeat, key_feat, key_low, random_dirs) * feature_scale
    dqkv_low = jnp.concatenate(
        [
            dquery.reshape(row_count, model_width),
            dkeys.reshape(row_count, model_width),
            dvalues.reshape(row_count, model_width),
        ],
        axis=1,
    ).astype(jnp.bfloat16)
    grad_bias_qkv = column_sum(dqkv_low)
    grad_weight_qkv = rows_product(token_low, dqkv_low)
    dtokens = dfirst + back_product(dqkv_low, back_qkv)
    group_sums = (
        lax.psum_scatter(grad_weight_qkv, "fsdp", scatter_dimension=0, tiled=True),
        lax.psum_scatter(grad_bias_qkv, "fsdp", scatter_dimension=0, tiled=True),
        lax.psum_scatter(grad_weight_proj, "fsdp", scatter_dimension=0, tiled=True),
        lax.psum_scatter(grad_bias_proj, "fsdp", scatter_dimension=0, tiled=True),
        lax.psum_scatter(grad_gain_attn, "fsdp", scatter_dimension=0, tiled=True),
        lax.psum_scatter(grad_shift_attn, "fsdp", scatter_dimension=0, tiled=True),
        lax.psum_scatter(grad_weight_inner, "fsdp", scatter_dimension=0, tiled=True),
        lax.psum_scatter(grad_bias_inner, "fsdp", scatter_dimension=0, tiled=True),
        lax.psum_scatter(grad_weight_outer, "fsdp", scatter_dimension=0, tiled=True),
        lax.psum_scatter(grad_bias_outer, "fsdp", scatter_dimension=0, tiled=True),
        lax.psum_scatter(grad_gain_ffn, "fsdp", scatter_dimension=0, tiled=True),
        lax.psum_scatter(grad_shift_ffn, "fsdp", scatter_dimension=0, tiled=True),
    )
    (
        sum_wqkv,
        sum_bqkv,
        sum_wproj,
        sum_bproj,
        sum_gattn,
        sum_sattn,
        sum_winner,
        sum_binner,
        sum_wouter,
        sum_bouter,
        sum_gffn,
        sum_sffn,
    ) = group_sums
    totals = lax.psum(
        (
            sum_wqkv,
            sum_bqkv,
            sum_wproj,
            sum_bproj,
            sum_gattn,
            sum_sattn,
            sum_winner,
            sum_binner,
            sum_wouter,
            sum_bouter,
            sum_gffn,
            sum_sffn,
        ),
        "replica",
    )
    out_rows = result.astype(jnp.bfloat16).reshape(groups, piece_rows, model_width)
    grad_rows = dtokens.astype(jnp.bfloat16).reshape(groups, piece_rows, model_width)
    back_out, back_grad = (
        lax.all_to_all(out_rows, "fsdp", split_axis=0, concat_axis=0, tiled=True),
        lax.all_to_all(grad_rows, "fsdp", split_axis=0, concat_axis=0, tiled=True),
    )
    inverse = jnp.zeros((groups,), jnp.int32).at[deal_row].set(lax.iota(jnp.int32, groups))
    layer_out = jnp.take(back_out, inverse, axis=0).reshape(row_count, model_width)
    tokens_grad = jnp.take(back_grad, inverse, axis=0).reshape(row_count, model_width)
    return (
        layer_out,
        tokens_grad,
        totals[0],
        totals[1],
        totals[2],
        totals[3],
        totals[4],
        totals[5],
        totals[6],
        totals[7],
        totals[8],
        totals[9],
        totals[10],
        totals[11],
    )


def solution(mesh):
    return jax.shard_map(
        body,
        mesh=mesh,
        in_specs=(
            P(("replica", "fsdp"), None),
            P(("replica", "fsdp"), None),
            P("fsdp", None),
            P("fsdp"),
            P("fsdp", None),
            P("fsdp"),
            P("fsdp"),
            P("fsdp"),
            P("fsdp", None),
            P("fsdp"),
            P("fsdp", None),
            P("fsdp"),
            P("fsdp"),
            P("fsdp"),
            P(),
            P("replica", "fsdp", None),
            P("replica", None),
        ),
        out_specs=(
            P(("replica", "fsdp"), None),
            P(("replica", "fsdp"), None),
            P("fsdp", None),
            P("fsdp"),
            P("fsdp", None),
            P("fsdp"),
            P("fsdp"),
            P("fsdp"),
            P("fsdp", None),
            P("fsdp"),
            P("fsdp", None),
            P("fsdp"),
            P("fsdp"),
            P("fsdp"),
        ),
        check_vma=False,
    )
```

profile of v0, /device:TPU:0, one launch (start us, length us, event | category | flops | bytes accessed | tf_op | source)
XLA Modules:
  0.0 745.2 jit_solution(5544804439539207280)
XLA Ops:
  14.0 7.4 all-to-all-start
  26.5 71.3 %all-reduce.19 = (bf16[2304]{0:T(1024)(128)(2,1)S(1)}, bf16[768]{0:T(1024)(128)(2,1)S(1)}, bf16[768]{0:T(1024)(128)(2,1)S(1)}, bf16[768]{0:T(1024)(128)(2,1)S(1)...) all-reduce(bf16[2304]{0:T(1024)(128)(2,1)S(1)} %dynamic-update-slic, ...), channel_id=1, replica_groups=mesh['replica'=2,'fsdp'=16] {'fsdp'}, use_global_device_ids=true, to_apply=%add | all-reduce | flops 9984 | bytes 39936
  101.6 4.3 all-to-all-start.2
  106.0 4.0 convolution_add_fusion
  117.2 5.0 fusion.35
  122.2 3.0 copy.65
  126.5 4.9 fusion.34
  136.1 4.3 fusion.4
  140.5 3.1 fusion.52
  144.9 6.1 fusion.68
  154.4 12.6 %all-gather.9.cloned.1.call-done = bf16[768,3072]{1,0:T(8,128)(2,1)} async-done(((bf16[48,3072]{1,0:T(8,128)(2,1)}), bf16[768,3072]{1,0:T(8,128)(2,1)}) %all-gather.9.cloned.1.call-update) | async-done | bytes 4718608 | tf_op jit(solution)/shard_map/all_gather | solution.py:93
  167.0 20.1 %multiply_convert_fusion = (bf16[512,3072]{1,0:T(8,128)(2,1)}, f32[512,3072]{1,0:T(8,128)}, f32[512,3072]{1,0:T(8,128)}) fusion(f32[3072]{0:T(1024)} %convert_element_type.179, bf16[768,3072]{1,0:T(8,128)(2,1)} %all-gather.9.cloned.1.call-done, f32[512,768]{1,0:T(8,128)S(1)} %get-tuple-element.80, f32[768]{0:T(1024)} %convert_element_type.177, ...), kind=kOutput, calls=%fused_computation.41 | convolution fusion | flops 2521694208 | bytes 22042624 | tf_op jit(solution)/shard_map/dot_general | solution.py:17
  187.1 33.7 %all-gather.11.cloned.1.call-done = bf16[3072,768]{1,0:T(8,128)(2,1)} async-done(((bf16[192,768]{1,0:T(8,128)(2,1)}), bf16[3072,768]{1,0:T(8,128)(2,1)}) %all-gather.11.cloned.1.call-update) | async-done | bytes 4718608 | tf_op jit(solution)/shard_map/all_gather | solution.py:95
  220.8 6.1 fusion.109
  235.3 9.1 %convert_reduce_fusion = (f32[3072]{0:T(1024)}, bf16[512,3072]{1,0:T(8,128)(2,1)S(1)}) fusion(f32[512,3072]{1,0:T(8,128)} %get-tuple-element.61, f32[512,3072]{1,0:T(8,128)} %get-tuple-element.81, f32[3072]{0:T(1024)S(1)} %copy-done.48, bf16[512,768]{1,0:T(8,128)(2,1)S(1)} %get-tuple-element.49, bf16[3072,768]{1,0:T(8,128)(2,1)S(1)} %copy-done.62), kind=kOutput, calls=%fused_computation.39 | convolution fusion | flops 2442654720 | bytes 21258240 | tf_op jit(solution)/shard_map/dot_general | solution.py:27
  244.4 3.7 multiply_reduce_fusion.2
  257.2 3.1 fusion
  260.3 4.6 fusion.55
  265.2 3.8 fusion.36
  280.0 5.1 bitcast_convert_fusion
  286.1 5.0 fusion.98
  291.8 7.2 fusion.99
  300.1 8.2 %fusion.114 = f32[3072,768]{1,0:T(8,128)} fusion(bf16[512,3072]{1,0:T(8,128)(2,1)} %get-tuple-element.60, bf16[512,768]{1,0:T(8,128)(2,1)S(1)} %copy-done.22), kind=kOutput, calls=%fused_computation.179 | convolution fusion | flops 2415919104 | bytes 13369344 | tf_op jit(solution)/shard_map/dot_general | solution.py:21
  308.3 3.8 all-to-all-start.1
  312.1 5.6 add_convert_fusion.1
  317.7 17.7 %all-to-all-done.1 = bf16[16,32,768]{2,1,0:T(8,128)(2,1)S(1)} async-done(((bf16[16,32,768]{2,1,0:T(8,128)(2,1)}), bf16[16,32,768]{2,1,0:T(8,128)(2,1)S(1)}, u32[]{:S(2)}, u32[]{:S(2)}) %all-to-all-start.1) | async-done | bytes 786464 | tf_op jit(solution)/shard_map/all_to_all | solution.py:281
  335.4 5.5 all-to-all-start.3
  341.0 85.3 %reduce-scatter.5.cloned.1.call-done = f32[48,2304]{1,0:T(8,128)} async-done(((f32[768,2304]{1,0:T(8,128)}), f32[48,2304]{1,0:T(8,128)}) %reduce-scatter.5.cloned.1.call-update) | async-done | bytes 442384 | tf_op jit(solution)/shard_map/reduce_scatter | solution.py:234
  426.3 115.0 %reduce-scatter.9.cloned.1.call-done = f32[48,3072]{1,0:T(8,128)} async-done(((f32[768,3072]{1,0:T(8,128)}), f32[48,3072]{1,0:T(8,128)}) %reduce-scatter.9.cloned.1.call-update) | async-done | bytes 589840 | tf_op jit(solution)/shard_map/reduce_scatter | solution.py:240
  541.3 115.0 %reduce-scatter.11.cloned.1.call-done = f32[192,768]{1,0:T(8,128)} async-done(((f32[3072,768]{1,0:T(8,128)}), f32[192,768]{1,0:T(8,128)}) %reduce-scatter.11.cloned.1.call-update) | async-done | bytes 589840 | tf_op jit(solution)/shard_map/reduce_scatter | solution.py:242
  662.0 60.3 %all-reduce.16 = (f32[2304]{0:T(1024)S(1)}, f32[768]{0:T(1024)S(1)}, f32[768]{0:T(1024)S(1)}, f32[768]{0:T(1024)S(1)}, f32[3072]{0:T(1024)S(1)}, /*index=5*/f32[...) all-reduce(f32[2304]{0:T(1024)S(1)} %convert_reduce_fusion.1, ...), channel_id=3, replica_groups=mesh['replica'=2,'fsdp'=16] {'fsdp'}, use_global_device_ids=true, to_apply=%region_19.21.clone | all-reduce | flops 9984 | bytes 79872
  722.9 5.5 all-reduce.17
  (292 shorter events, 76.6 us)
Async XLA Ops:
  7.2 98.8 %all-gather.5.cloned.1.call-start = ((), (), s32[]{:S(2)}) async-start(), calls=%async_computation.8 | async-start | bytes 3760128 | tf_op jit(solution)/shard_map/all_gather | solution.py:87
  7.9 143.0 %all-gather.7.cloned.1.call-start = ((), (), s32[]{:S(2)}) async-start(), calls=%async_computation.9 | async-start | bytes 1253376 | tf_op jit(solution)/shard_map/all_gather | solution.py:89
  8.7 158.3 %all-gather.9.cloned.1.call-start = ((), (), s32[]{:S(2)}) async-start(), calls=%async_computation.10 | async-start | bytes 5013504 | tf_op jit(solution)/shard_map/all_gather | solution.py:93
  10.7 13.8 %copy-start.63 = (bf16[48]{0:T(256)(128)(2,1)S(1)}, bf16[48]{0:T(256)(128)(2,1)}, u32[]{:S(2)}) copy-start(bf16[48]{0:T(256)(128)(2,1)} %param.32) | copy-start | bytes 292
  10.7 14.1 %copy-start.64 = (bf16[48]{0:T(256)(128)(2,1)S(1)}, bf16[48]{0:T(256)(128)(2,1)}, u32[]{:S(2)}) copy-start(bf16[48]{0:T(256)(128)(2,1)} %param.30) | copy-start | bytes 292
  10.7 14.3 %copy-start.65 = (bf16[48]{0:T(256)(128)(2,1)S(1)}, bf16[48]{0:T(256)(128)(2,1)}, u32[]{:S(2)}) copy-start(bf16[48]{0:T(256)(128)(2,1)} %param.25) | copy-start | bytes 292
  10.8 14.5 %copy-start.66 = (bf16[48]{0:T(256)(128)(2,1)S(1)}, bf16[48]{0:T(256)(128)(2,1)}, u32[]{:S(2)}) copy-start(bf16[48]{0:T(256)(128)(2,1)} %param.26) | copy-start | bytes 292
  10.8 14.7 %copy-start.67 = (bf16[48]{0:T(256)(128)(2,1)S(1)}, bf16[48]{0:T(256)(128)(2,1)}, u32[]{:S(2)}) copy-start(bf16[48]{0:T(256)(128)(2,1)} %param.24) | copy-start | bytes 292
  10.8 14.9 %copy-start.68 = (bf16[48]{0:T(256)(128)(2,1)S(1)}, bf16[48]{0:T(256)(128)(2,1)}, u32[]{:S(2)}) copy-start(bf16[48]{0:T(256)(128)(2,1)} %param.31) | copy-start | bytes 292
  10.8 15.2 %copy-start.69 = (bf16[192]{0:T(256)(128)(2,1)S(1)}, bf16[192]{0:T(256)(128)(2,1)}, u32[]{:S(2)}) copy-start(bf16[192]{0:T(256)(128)(2,1)} %param.28) | copy-start | bytes 1156
  10.8 15.4 %copy-start.70 = (bf16[144]{0:T(256)(128)(2,1)S(1)}, bf16[144]{0:T(256)(128)(2,1)}, u32[]{:S(2)}) copy-start(bf16[144]{0:T(256)(128)(2,1)} %param.22) | copy-start | bytes 868
  10.8 89.9 %copy-start.71 = (s32[1,1,4]{2,1,0:T(1,128)S(1)}, s32[1,1,4]{2,1,0:T(1,128)}, u32[]{:S(2)}) copy-start(s32[1,1,4]{2,1,0:T(1,128)} %param.34) | copy-start | bytes 52
  14.0 87.6 %all-to-all-start = ((bf16[16,32,768]{2,1,0:T(8,128)(2,1)}), bf16[16,32,768]{2,1,0:T(8,128)(2,1)S(1)}, u32[]{:S(2)}, u32[]{:S(2)}) async-start(bf16[16,32,768]{2,1,0:T(8,128)(2,1)} %get-tuple-element.72), calls=%async_computation | async-start | bytes 1572864 | tf_op jit(solution)/shard_map/all_to_all | solution.py:81
  21.4 199.4 %all-gather.11.cloned.1.call-start = ((), (), s32[]{:S(2)}) async-start(), calls=%async_computation.11 | async-start | bytes 5013504 | tf_op jit(solution)/shard_map/all_gather | solution.py:95
  101.6 126.8 %all-to-all-start.2 = ((bf16[16,32,768]{2,1,0:T(8,128)(2,1)}), bf16[16,32,768]{2,1,0:T(8,128)(2,1)}, u32[]{:S(2)}, u32[]{:S(2)}) async-start(bf16[16,32,768]{2,1,0:T(8,128)(2,1)} %get-tuple-element.71), calls=%async_computation.2 | async-start | bytes 1572864 | tf_op jit(solution)/shard_map/all_to_all | solution.py:82
  105.9 235.1 %reduce-scatter.7.cloned.1.call-start = ((), (), s32[]{:S(2)}) async-start(), calls=%async_computation.13 | async-start | bytes 2506752 | tf_op jit(solution)/shard_map/reduce_scatter | solution.py:236
  153.4 67.3 %copy-start.39 = (f32[512]{0:T(512)}, f32[512]{0:T(512)S(1)}, u32[]{:S(2)}) copy-start(f32[512]{0:T(512)S(1)} %broadcast_multiply_fusion.3) | copy-start | bytes 6148
  154.3 32.7 %copy-start.50 = (f32[512]{0:T(512)}, f32[512]{0:T(512)S(1)}, u32[]{:S(2)}) copy-start(f32[512]{0:T(512)S(1)} %fusion.93) | copy-start | bytes 6148
  264.9 161.3 %reduce-scatter.5.cloned.1.call-start = ((), (), s32[]{:S(2)}) async-start(), calls=%async_computation.12 | async-start | bytes 7520256 | tf_op jit(solution)/shard_map/reduce_scatter | solution.py:234
  272.9 12.3 %copy-start.11 = (bf16[512,12,64]{0,2,1:T(8,128)(2,1)}, bf16[512,12,64]{0,2,1:T(8,128)(2,1)S(1)}, u32[]{:S(2)}) copy-start(bf16[512,12,64]{0,2,1:T(8,128)(2,1)S(1)} %fusion.61) | copy-start | bytes 2359300
  291.1 250.2 %reduce-scatter.9.cloned.1.call-start = ((), (), s32[]{:S(2)}) async-start(), calls=%async_computation.14 | async-start | bytes 10027008 | tf_op jit(solution)/shard_map/reduce_scatter | solution.py:240
  299.0 357.3 %reduce-scatter.11.cloned.1.call-start = ((), (), s32[]{:S(2)}) async-start(), calls=%async_computation.15 | async-start | bytes 10027008 | tf_op jit(solution)/shard_map/reduce_scatter | solution.py:242
  308.3 27.1 %all-to-all-start.1 = ((bf16[16,32,768]{2,1,0:T(8,128)(2,1)}), bf16[16,32,768]{2,1,0:T(8,128)(2,1)S(1)}, u32[]{:S(2)}, u32[]{:S(2)}) async-start(bf16[16,32,768]{2,1,0:T(8,128)(2,1)} %bitcast.192), calls=%async_computation.1 | async-start | bytes 1572864 | tf_op jit(solution)/shard_map/all_to_all | solution.py:281
  317.7 340.6 %copy-start.73 = (s32[1,16]{1,0:T(1,128)S(1)}, s32[1,16]{1,0:T(1,128)}, u32[]{:S(2)}) copy-start(s32[1,16]{1,0:T(1,128)} %param.35) | copy-start | bytes 196
  317.7 342.7 %copy-start.14 = (bf16[512,12,64]{0,2,1:T(8,128)(2,1)S(1)}, bf16[512,12,64]{0,2,1:T(8,128)(2,1)}, u32[]{:S(2)}) copy-start(bf16[512,12,64]{0,2,1:T(8,128)(2,1)} %copy-done.13) | copy-start | bytes 2359300
  335.4 326.5 %copy-start.44 = (f32[768]{0:T(1024)S(1)}, f32[768]{0:T(1024)}, u32[]{:S(2)}) copy-start(f32[768]{0:T(1024)} %get-tuple-element.17) | copy-start | bytes 9220
  335.4 326.6 %copy-start.45 = (f32[768]{0:T(1024)S(1)}, f32[768]{0:T(1024)}, u32[]{:S(2)}) copy-start(f32[768]{0:T(1024)} %get-tuple-element.48) | copy-start | bytes 9220
  335.4 326.6 %copy-start.49 = (f32[3072]{0:T(1024)S(1)}, f32[3072]{0:T(1024)}, u32[]{:S(2)}) copy-start(f32[3072]{0:T(1024)} %get-tuple-element.50) | copy-start | bytes 36868
  335.4 326.6 %copy-start.58 = (f32[768]{0:T(1024)S(1)}, f32[768]{0:T(1024)}, u32[]{:S(2)}) copy-start(f32[768]{0:T(1024)} %get-tuple-element.15) | copy-start | bytes 9220
  335.4 326.6 %copy-start.59 = (f32[768]{0:T(1024)S(1)}, f32[768]{0:T(1024)}, u32[]{:S(2)}) copy-start(f32[768]{0:T(1024)} %get-tuple-element.19) | copy-start | bytes 9220
  335.4 393.6 %all-to-all-start.3 = ((bf16[16,32,768]{2,1,0:T(8,128)(2,1)}), bf16[16,32,768]{2,1,0:T(8,128)(2,1)S(1)}, u32[]{:S(2)}, u32[]{:S(2)}) async-start(bf16[16,32,768]{2,1,0:T(8,128)(2,1)} %bitcast.200), calls=%async_computation.3 | async-start | bytes 1572864 | tf_op jit(solution)/shard_map/all_to_all | solution.py:282
  340.9 390.1 %all-reduce.22.cloned.1.call-start = ((), (), s32[]{:S(2)}) async-start(), calls=%async_computation.16 | async-start | bytes 3538944 | tf_op jit(solution)/shard_map/psum | solution.py:261
  (65 other events, 241.5 us)
Sparse Core Ops, SparseCore 0:
  10.3 59.1 all-gather.4
  71.8 37.0 all-gather.6
  111.2 55.7 all-gather.8
  169.1 51.6 all-gather.10
  265.1 67.9 reduce-scatter.6
  337.0 89.2 reduce-scatter.4
  430.4 110.8 reduce-scatter.8
  545.4 110.8 reduce-scatter.10
  658.8 55.4 all-reduce.21
where the time goes:
time: 753 us; the launch traced here: 745 us
  waiting for transfers between devices  382 us (51%)
  blocking collectives  137 us (18%)
  matrix products  124 us (16%)
  local copies, waits for them, and re-layouts  38.5 us (5%)
  other arithmetic  22.6 us (3%)
  starting transfers between devices  21.8 us (3%)
  between operations  19.2 us (3%)
    unnamed x2, blocking collectives  132 us
    reduce_scatter x1, waiting for transfers between devices, body(): lax.psum_scatter(grad_weight_inner, 'fsdp', scatter_dimension=0, tiled=True)  115 us
    reduce_scatter x1, waiting for transfers between devices, body(): lax.psum_scatter(grad_weight_outer, 'fsdp', scatter_dimension=0, tiled=True)  115 us
    reduce_scatter x1, waiting for transfers between devices, body(): lax.psum_scatter(grad_weight_qkv, 'fsdp', scatter_dimension=0, tiled=True)  85.3 us
    all_gather x1, waiting for transfers between devices, body(): lax.all_gather(outer_weight, 'fsdp', axis=0, tiled=True)  33.7 us
    dot_general x4, matrix products, matrix_product(): return jnp.dot(left, right, preferred_element_type=jnp.float32)  32.7 us
    unnamed x197, local copies, waits for them, and re-layouts  24.3 us
    dot_general x4, matrix products, rows_product(): lax.dot_general(left, right, (((0,), (0,)), ((), ())), preferred_element_...  22.6 us
  transfers between devices with their start and end apart: 13, of which 6 were waited for; matrix products, arithmetic and copies ran while one was open for 17% of the time, Pallas kernels for 0%

commit v1 on v0

--- a/solution.py
+++ b/solution.py
@@ -1,3 +1,4 @@
+import functools
 from functools import partial
 import jax
 import jax.numpy as jnp
@@ -5,6 +6,40 @@
 from jax.sharding import PartitionSpec as P
 
 EPSILON = 1e-06
+
+
+def _get_rails(obj, axis_tag):
+    heap = []
+    i = 0
+    outer, r2, step_out = (lax.axis_size(axis_tag), lax.axis_index(axis_tag), obj.shape[0])
+    while i < outer:
+        heap.append((i, (i + 1) % outer))
+        i = i + 1
+    buffer = []
+    i = 0
+    while i < outer:
+        buffer.append((i, (i - 1) % outer))
+        i = i + 1
+    arr_now = jnp.zeros((*obj.shape[:0], outer * step_out, *obj.shape[1:]), obj.dtype)
+    ready = far_arr = obj
+    arr_now = lax.dynamic_update_slice_in_dim(arr_now, obj, r2 * step_out, axis=0)
+    dev = 1
+    k_now = outer // 2
+    while dev < k_now + 1:
+        ready = lax.ppermute(ready, axis_tag, heap)
+        arr_now = lax.dynamic_update_slice_in_dim(
+            arr_now, ready, (r2 - dev) % outer * step_out, axis=0
+        )
+        if dev < outer - k_now:
+            far_arr = lax.ppermute(far_arr, axis_tag, buffer)
+            arr_now = lax.dynamic_update_slice_in_dim(
+                arr_now, far_arr, (r2 + dev) % outer * step_out, axis=0
+            )
+        dev += 1
+    return arr_now
+
+
+touch_the_sections = functools.partial(_get_rails, axis_tag="fsdp")
 
 
 def layer_norm(summed, gain_vec, shift_vec):
@@ -92,7 +127,7 @@
         lax.all_gather(attn_shift, "fsdp", axis=0, tiled=True),
         lax.all_gather(inner_weight, "fsdp", axis=0, tiled=True),
         lax.all_gather(inner_bias, "fsdp", axis=0, tiled=True),
-        lax.all_gather(outer_weight, "fsdp", axis=0, tiled=True),
+        touch_the_sections(outer_weight),
         lax.all_gather(outer_bias, "fsdp", axis=0, tiled=True),
         lax.all_gather(ffn_gain, "fsdp", axis=0, tiled=True),
         lax.all_gather(ffn_shift, "fsdp", axis=0, tiled=True),

time: 753 us -> 785 us (1.042)
  waiting for transfers between devices: 382 us -> 351 us
  starting transfers between devices: 21.8 us -> 44.6 us
  blocking collectives: 137 us -> 155 us
  local copies, waits for them, and re-layouts: 38.5 us -> 52.2 us
  matrix products: 124 us -> 132 us
    ppermute x0 -> x15, waiting for transfers between devices: none -> 40.5 us  [the longest x7 35.1 us: _get_rails(): far_arr = lax.ppermute(far_arr, axis_tag, buffer)]
    all_gather x1, waiting for transfers between devices: 33.7 us -> 0.01 us  [body(): lax.all_gather(outer_weight, 'fsdp', axis=0, tiled=True)]
    ppermute x0 -> x15, starting transfers between devices: none -> 29 us  [the longest x7 27.8 us: _get_rails(): far_arr = lax.ppermute(far_arr, axis_tag, buffer)]
    all_to_all x0 -> x1, blocking collectives: none -> 26.9 us  [body(): lax.all_to_all(grad_rows, 'fsdp', split_axis=0, concat_axis=0, tiled=True)]
    all_to_all x1, waiting for transfers between devices: 17.7 us -> 0.01 us  [body(): lax.all_to_all(out_rows, 'fsdp', split_axis=0, concat_axis=0, tiled=True)]
    all_gather x1, waiting for transfers between devices: 12.6 us -> 0.01 us  [body(): lax.all_gather(inner_weight, 'fsdp', axis=0, tiled=True)]
    dynamic_update_slice x0 -> x16, local copies, waits for them, and re-layouts: none -> 11.8 us  [the longest x8 5.9 us: _get_rails(): lax.dynamic_update_slice_in_dim(arr_now, ready, (r2 - dev) % outer * step...]
    unnamed x2, blocking collectives: 132 us -> 123 us
  transfers between devices with their start and end apart: 13 -> 27, of which waited for: 6 -> 11; matrix products, arithmetic and copies ran while one was open for 17% -> 21% of each run, Pallas kernels for 0% -> 0%
where the time goes in v1:
time: 785 us; the launch traced here: 776 us
  waiting for transfers between devices  351 us (45%)
  blocking collectives  155 us (20%)
  matrix products  132 us (17%)
  local copies, waits for them, and re-layouts  52.2 us (7%)
  starting transfers between devices  44.6 us (6%)
  other arithmetic  22.2 us (3%)
  between operations  19 us (2%)
    unnamed x2, blocking collectives  123 us
    reduce_scatter x1, waiting for transfers between devices, body(): lax.psum_scatter(grad_weight_outer, 'fsdp', scatter_dimension=0, tiled=True)  115 us
    reduce_scatter x1, waiting for transfers between devices, body(): lax.psum_scatter(grad_weight_inner, 'fsdp', scatter_dimension=0, tiled=True)  115 us
    reduce_scatter x1, waiting for transfers between devices, body(): lax.psum_scatter(grad_weight_qkv, 'fsdp', scatter_dimension=0, tiled=True)  77.4 us
    ppermute x7, waiting for transfers between devices, _get_rails(): far_arr = lax.ppermute(far_arr, axis_tag, buffer)  35.1 us
    dot_general x4, matrix products, matrix_product(): return jnp.dot(left, right, preferred_element_type=jnp.float32)  32.4 us
    ppermute x7, starting transfers between devices, _get_rails(): far_arr = lax.ppermute(far_arr, axis_tag, buffer)  27.8 us
    all_to_all x1, blocking collectives, body(): lax.all_to_all(grad_rows, 'fsdp', split_axis=0, concat_axis=0, tiled=True)  26.9 us
  transfers between devices with their start and end apart: 27, of which 11 were waited for; matrix products, arithmetic and copies ran while one was open for 21% of the time, Pallas kernels for 0%

profile of v1, /device:TPU:0, one launch (start us, length us, event | category | flops | bytes accessed | tf_op | source)
XLA Modules:
  0.0 776.1 jit_solution(18402903235834963941)
XLA Ops:
  10.0 5.0 collective-permute-start.1
  21.1 6.9 all-to-all-start
  28.8 4.3 collective-permute-start.3
  33.9 16.8 %collective-permute-done.3 = bf16[192,768]{1,0:T(8,128)(2,1)S(1)} collective-permute-done((bf16[192,768]{1,0:T(8,128)(2,1)S(1)}, bf16[192,768]{1,0:T(8,128)(2,1)S(1)}, u32[]{:S(2)}, u32[]{:S(2)}) %collective-permute-start.3) | collective-permute-done | bytes 294944 | tf_op jit(solution)/shard_map/ppermute | solution.py:34
  50.7 4.6 collective-permute-start.5
  63.0 62.3 %all-reduce.19 = (bf16[2304]{0:T(1024)(128)(2,1)S(1)}, bf16[768]{0:T(1024)(128)(2,1)S(1)}, bf16[768]{0:T(1024)(128)(2,1)S(1)}, bf16[768]{0:T(1024)(128)(2,1)S(1)...) all-reduce(bf16[2304]{0:T(1024)(128)(2,1)S(1)} %dynamic-update-slic, ...), channel_id=1, replica_groups=mesh['replica'=2,'fsdp'=16] {'fsdp'}, use_global_device_ids=true, to_apply=%add | all-reduce | flops 9984 | bytes 39936
  131.8 6.7 collective-permute-done.7
  138.5 4.6 collective-permute-start.9
  145.3 4.9 collective-permute-done.9
  150.1 4.6 collective-permute-start.11
  161.4 4.6 collective-permute-start.13
  188.6 4.9 fusion.34
  203.0 4.9 fusion.35
  212.2 5.3 fusion.52
  222.4 6.0 fusion.68
  231.9 19.7 %multiply_convert_fusion = (bf16[512,3072]{1,0:T(8,128)(2,1)S(1)}, f32[512,3072]{1,0:T(8,128)}, f32[512,3072]{1,0:T(8,128)}) fusion(f32[3072]{0:T(1024)} %convert_element_type.179, bf16[768,3072]{1,0:T(8,128)(2,1)} %all-gather.9.cloned.1.call-done, f32[512,768]{1,0:T(8,128)S(1)} %get-tuple-element.80, f32[768]{0:T(1024)} %convert_element_type.177, ...), kind=kOutput, calls=%fused_computation.41 | convolution fusion | flops 2521694208 | bytes 22042624 | tf_op jit(solution)/shard_map/dot_general | solution.py:52
  251.7 6.2 fusion.109
  267.2 9.3 %convert_reduce_fusion = (f32[3072]{0:T(1024)}, bf16[512,3072]{1,0:T(8,128)(2,1)S(1)}) fusion(f32[512,3072]{1,0:T(8,128)} %get-tuple-element.61, f32[512,3072]{1,0:T(8,128)} %get-tuple-element.81, f32[3072]{0:T(1024)} %convert_element_type.179, bf16[512,768]{1,0:T(8,128)(2,1)S(1)} %get-tuple-element.49, bf16[3072,768]{1,0:T(8,128)(2,1)} %all-gather.11.cloned.1.call-done), kind=kOutput, calls=%fused_computation.39 | convolution fusion | flops 2442654720 | bytes 21258240 | tf_op jit(solution)/shard_map/dot_general | solution.py:62
  276.6 7.2 multiply_reduce_fusion.2
  291.3 4.5 fusion.38
  296.5 6.3 fusion.111
  315.6 5.3 bitcast_convert_fusion
  321.8 5.0 fusion.98
  326.9 8.4 %fusion.114 = f32[3072,768]{1,0:T(8,128)} fusion(bf16[512,3072]{1,0:T(8,128)(2,1)} %copy-done.76, bf16[512,768]{1,0:T(8,128)(2,1)} %copy-done.26), kind=kOutput, calls=%fused_computation.195 | convolution fusion | flops 2415919104 | bytes 13369344 | tf_op jit(solution)/shard_map/dot_general | solution.py:56
  336.0 7.2 fusion.99
  344.6 4.3 add_convert_fusion.1
  348.9 26.9 %all_to_all.20 = bf16[16,32,768]{2,1,0:T(8,128)(2,1)S(1)} all-to-all(bf16[16,32,768]{2,1,0:T(8,128)(2,1)S(1)} %bitcast.197), channel_id=1, replica_groups=mesh['replica'=2,'fsdp'=16] {'fsdp'}, dimensions={0} | all-to-all | bytes 1572864 | tf_op jit(solution)/shard_map/all_to_all | solution.py:317
  380.0 77.4 %reduce-scatter.5.cloned.1.call-done = f32[48,2304]{1,0:T(8,128)} async-done(((f32[768,2304]{1,0:T(8,128)}), f32[48,2304]{1,0:T(8,128)}) %reduce-scatter.5.cloned.1.call-update) | async-done | bytes 442384 | tf_op jit(solution)/shard_map/reduce_scatter | solution.py:269
  457.4 115.0 %reduce-scatter.11.cloned.1.call-done = f32[192,768]{1,0:T(8,128)} async-done(((f32[3072,768]{1,0:T(8,128)}), f32[192,768]{1,0:T(8,128)}) %reduce-scatter.11.cloned.1.call-update) | async-done | bytes 589840 | tf_op jit(solution)/shard_map/reduce_scatter | solution.py:277
  572.4 115.0 %reduce-scatter.9.cloned.1.call-done = f32[48,3072]{1,0:T(8,128)} async-done(((f32[768,3072]{1,0:T(8,128)}), f32[48,3072]{1,0:T(8,128)}) %reduce-scatter.9.cloned.1.call-update) | async-done | bytes 589840 | tf_op jit(solution)/shard_map/reduce_scatter | solution.py:275
  693.1 60.3 %all-reduce.16 = (f32[2304]{0:T(1024)S(1)}, f32[768]{0:T(1024)S(1)}, f32[768]{0:T(1024)S(1)}, f32[768]{0:T(1024)S(1)}, f32[3072]{0:T(1024)S(1)}, /*index=5*/f32[...) all-reduce(f32[2304]{0:T(1024)S(1)} %convert_reduce_fusion.1, ...), channel_id=3, replica_groups=mesh['replica'=2,'fsdp'=16] {'fsdp'}, use_global_device_ids=true, to_apply=%region_19.21.clone | all-reduce | flops 9984 | bytes 79872
  754.0 5.7 all-reduce.17
  (332 shorter events, 126.9 us)
Async XLA Ops:
  7.2 173.7 %all-gather.5.cloned.1.call-start = ((), (), s32[]{:S(2)}) async-start(), calls=%async_computation.8 | async-start | bytes 3760128 | tf_op jit(solution)/shard_map/all_gather | solution.py:122
  7.9 220.5 %all-gather.7.cloned.1.call-start = ((), (), s32[]{:S(2)}) async-start(), calls=%async_computation.9 | async-start | bytes 1253376 | tf_op jit(solution)/shard_map/all_gather | solution.py:124
  8.7 223.2 %all-gather.9.cloned.1.call-start = ((), (), s32[]{:S(2)}) async-start(), calls=%async_computation.10 | async-start | bytes 5013504 | tf_op jit(solution)/shard_map/all_gather | solution.py:128
  9.4 10.3 %collective-permute-start = (bf16[192,768]{1,0:T(8,128)(2,1)}, bf16[192,768]{1,0:T(8,128)(2,1)S(1)}, u32[]{:S(2)}, u32[]{:S(2)}) collective-permute-start(bf16[192,768]{1,0:T(8,128)(2,1)} %param.29), channel_id=1, source_target_pairs={{0,1},{1,2},{2,3},{3,4},{4,5},{5,6},{6,7},{7,8},{8,9},{9,10},{10,1... | collective-permute-start | bytes 884744 | tf_op jit(solution)/shard_map/ppermute | solution.py:29
  10.0 18.8 %collective-permute-start.1 = (bf16[192,768]{1,0:T(8,128)(2,1)}, bf16[192,768]{1,0:T(8,128)(2,1)S(1)}, u32[]{:S(2)}, u32[]{:S(2)}) collective-permute-start(bf16[192,768]{1,0:T(8,128)(2,1)} %param.29), channel_id=1, source_target_pairs={{0,15},{1,0},{2,1},{3,2},{4,3},{5,4},{6,5},{7,6},{8,7},{9,8},{10,9... | collective-permute-start | bytes 884744 | tf_op jit(solution)/shard_map/ppermute | solution.py:34
  19.7 13.6 %collective-permute-start.2 = (bf16[192,768]{1,0:T(8,128)(2,1)S(1)}, bf16[192,768]{1,0:T(8,128)(2,1)S(1)}, u32[]{:S(2)}, u32[]{:S(2)}) collective-permute-start(bf16[192,768]{1,0:T(8,128)(2,1)S(1)} %collective-permute-done), channel_id=1, source_target_pairs={{0,1},{1,2},{2,3},{3,4},{4,5},{5,6},{6,7},{7,8},{8,9},{9,10},{10,1... | collective-permute-start | bytes 884744 | tf_op jit(solution)/shard_map/ppermute | solution.py:29
  21.1 155.4 %all-to-all-start = ((bf16[16,32,768]{2,1,0:T(8,128)(2,1)}), bf16[16,32,768]{2,1,0:T(8,128)(2,1)S(1)}, u32[]{:S(2)}, u32[]{:S(2)}) async-start(bf16[16,32,768]{2,1,0:T(8,128)(2,1)} %get-tuple-element.72), calls=%async_computation | async-start | bytes 1572864 | tf_op jit(solution)/shard_map/all_to_all | solution.py:116
  28.0 239.2 %all-gather.11.cloned.1.call-start = ((), (), s32[]{:S(2)}) async-start(), calls=%async_computation.11 | async-start | bytes 5013504 | tf_op jit(solution)/shard_map/all_gather | solution.py:208
  28.8 21.9 %collective-permute-start.3 = (bf16[192,768]{1,0:T(8,128)(2,1)S(1)}, bf16[192,768]{1,0:T(8,128)(2,1)S(1)}, u32[]{:S(2)}, u32[]{:S(2)}) collective-permute-start(bf16[192,768]{1,0:T(8,128)(2,1)S(1)} %collective-permute-done.1), channel_id=1, source_target_pairs={{0,15},{1,0},{2,1},{3,2},{4,3},{5,4},{6,5},{7,6},{8,7},{9,8},{10,9... | collective-permute-start | bytes 884744 | tf_op jit(solution)/shard_map/ppermute | solution.py:34
  33.3 22.1 %collective-permute-start.4 = (bf16[192,768]{1,0:T(8,128)(2,1)S(1)}, bf16[192,768]{1,0:T(8,128)(2,1)S(1)}, u32[]{:S(2)}, u32[]{:S(2)}) collective-permute-start(bf16[192,768]{1,0:T(8,128)(2,1)S(1)} %collective-permute-done.2), channel_id=1, source_target_pairs={{0,1},{1,2},{2,3},{3,4},{4,5},{5,6},{6,7},{7,8},{8,9},{9,10},{10,1... | collective-permute-start | bytes 884744 | tf_op jit(solution)/shard_map/ppermute | solution.py:29
  50.7 78.4 %collective-permute-start.5 = (bf16[192,768]{1,0:T(8,128)(2,1)S(1)}, bf16[192,768]{1,0:T(8,128)(2,1)S(1)}, u32[]{:S(2)}, u32[]{:S(2)}) collective-permute-start(bf16[192,768]{1,0:T(8,128)(2,1)S(1)} %collective-permute-done.3), channel_id=1, source_target_pairs={{0,15},{1,0},{2,1},{3,2},{4,3},{5,4},{6,5},{7,6},{8,7},{9,8},{10,9... | collective-permute-start | bytes 884744 | tf_op jit(solution)/shard_map/ppermute | solution.py:34
  55.3 74.5 %collective-permute-start.6 = (bf16[192,768]{1,0:T(8,128)(2,1)S(1)}, bf16[192,768]{1,0:T(8,128)(2,1)S(1)}, u32[]{:S(2)}, u32[]{:S(2)}) collective-permute-start(bf16[192,768]{1,0:T(8,128)(2,1)S(1)} %collective-permute-done.4), channel_id=1, source_target_pairs={{0,1},{1,2},{2,3},{3,4},{4,5},{5,6},{6,7},{7,8},{8,9},{9,10},{10,1... | collective-permute-start | bytes 884744 | tf_op jit(solution)/shard_map/ppermute | solution.py:29
  129.1 9.4 %collective-permute-start.7 = (bf16[192,768]{1,0:T(8,128)(2,1)S(1)}, bf16[192,768]{1,0:T(8,128)(2,1)S(1)}, u32[]{:S(2)}, u32[]{:S(2)}) collective-permute-start(bf16[192,768]{1,0:T(8,128)(2,1)S(1)} %collective-permute-done.5), channel_id=1, source_target_pairs={{0,15},{1,0},{2,1},{3,2},{4,3},{5,4},{6,5},{7,6},{8,7},{9,8},{10,9... | collective-permute-start | bytes 884744 | tf_op jit(solution)/shard_map/ppermute | solution.py:34
  129.8 14.0 %collective-permute-start.8 = (bf16[192,768]{1,0:T(8,128)(2,1)S(1)}, bf16[192,768]{1,0:T(8,128)(2,1)S(1)}, u32[]{:S(2)}, u32[]{:S(2)}) collective-permute-start(bf16[192,768]{1,0:T(8,128)(2,1)S(1)} %collective-permute-done.6), channel_id=1, source_target_pairs={{0,1},{1,2},{2,3},{3,4},{4,5},{5,6},{6,7},{7,8},{8,9},{9,10},{10,1... | collective-permute-start | bytes 884744 | tf_op jit(solution)/shard_map/ppermute | solution.py:29
  138.5 11.7 %collective-permute-start.9 = (bf16[192,768]{1,0:T(8,128)(2,1)S(1)}, bf16[192,768]{1,0:T(8,128)(2,1)S(1)}, u32[]{:S(2)}, u32[]{:S(2)}) collective-permute-start(bf16[192,768]{1,0:T(8,128)(2,1)S(1)} %collective-permute-done.7), channel_id=1, source_target_pairs={{0,15},{1,0},{2,1},{3,2},{4,3},{5,4},{6,5},{7,6},{8,7},{9,8},{10,9... | collective-permute-start | bytes 884744 | tf_op jit(solution)/shard_map/ppermute | solution.py:34
  143.8 12.5 %collective-permute-start.10 = (bf16[192,768]{1,0:T(8,128)(2,1)S(1)}, bf16[192,768]{1,0:T(8,128)(2,1)S(1)}, u32[]{:S(2)}, u32[]{:S(2)}) collective-permute-start(bf16[192,768]{1,0:T(8,128)(2,1)S(1)} %collective-permute-done.8), channel_id=1, source_target_pairs={{0,1},{1,2},{2,3},{3,4},{4,5},{5,6},{6,7},{7,8},{8,9},{9,10},{10,1... | collective-permute-start | bytes 884744 | tf_op jit(solution)/shard_map/ppermute | solution.py:29
  150.1 11.3 %collective-permute-start.11 = (bf16[192,768]{1,0:T(8,128)(2,1)S(1)}, bf16[192,768]{1,0:T(8,128)(2,1)S(1)}, u32[]{:S(2)}, u32[]{:S(2)}) collective-permute-start(bf16[192,768]{1,0:T(8,128)(2,1)S(1)} %collective-permute-done.9), channel_id=1, source_target_pairs={{0,15},{1,0},{2,1},{3,2},{4,3},{5,4},{6,5},{7,6},{8,7},{9,8},{10,9... | collective-permute-start | bytes 884744 | tf_op jit(solution)/shard_map/ppermute | solution.py:34
  156.3 10.4 %collective-permute-start.12 = (bf16[192,768]{1,0:T(8,128)(2,1)S(1)}, bf16[192,768]{1,0:T(8,128)(2,1)S(1)}, u32[]{:S(2)}, u32[]{:S(2)}) collective-permute-start(bf16[192,768]{1,0:T(8,128)(2,1)S(1)} %collective-permute-done.10), channel_id=1, source_target_pairs={{0,1},{1,2},{2,3},{3,4},{4,5},{5,6},{6,7},{7,8},{8,9},{9,10},{10,1... | collective-permute-start | bytes 884744 | tf_op jit(solution)/shard_map/ppermute | solution.py:29
  161.4 10.0 %collective-permute-start.13 = (bf16[192,768]{1,0:T(8,128)(2,1)S(1)}, bf16[192,768]{1,0:T(8,128)(2,1)S(1)}, u32[]{:S(2)}, u32[]{:S(2)}) collective-permute-start(bf16[192,768]{1,0:T(8,128)(2,1)S(1)} %collective-permute-done.11), channel_id=1, source_target_pairs={{0,15},{1,0},{2,1},{3,2},{4,3},{5,4},{6,5},{7,6},{8,7},{9,8},{10,9... | collective-permute-start | bytes 884744 | tf_op jit(solution)/shard_map/ppermute | solution.py:34
  166.7 9.0 %collective-permute-start.14 = (bf16[192,768]{1,0:T(8,128)(2,1)S(1)}, bf16[192,768]{1,0:T(8,128)(2,1)S(1)}, u32[]{:S(2)}, u32[]{:S(2)}) collective-permute-start(bf16[192,768]{1,0:T(8,128)(2,1)S(1)} %collective-permute-done.12), channel_id=1, source_target_pairs={{0,1},{1,2},{2,3},{3,4},{4,5},{5,6},{6,7},{7,8},{8,9},{9,10},{10,1... | collective-permute-start | bytes 884744 | tf_op jit(solution)/shard_map/ppermute | solution.py:29
  176.5 82.8 %all-to-all-start.2 = ((bf16[16,32,768]{2,1,0:T(8,128)(2,1)}), bf16[16,32,768]{2,1,0:T(8,128)(2,1)}, u32[]{:S(2)}, u32[]{:S(2)}) async-start(bf16[16,32,768]{2,1,0:T(8,128)(2,1)} %get-tuple-element.71), calls=%async_computation.2 | async-start | bytes 1572864 | tf_op jit(solution)/shard_map/all_to_all | solution.py:117
  180.8 199.1 %reduce-scatter.7.cloned.1.call-start = ((), (), s32[]{:S(2)}) async-start(), calls=%async_computation.13 | async-start | bytes 2506752 | tf_op jit(solution)/shard_map/reduce_scatter | solution.py:271
  296.4 160.9 %reduce-scatter.5.cloned.1.call-start = ((), (), s32[]{:S(2)}) async-start(), calls=%async_computation.12 | async-start | bytes 7520256 | tf_op jit(solution)/shard_map/reduce_scatter | solution.py:269
  326.8 245.6 %reduce-scatter.11.cloned.1.call-start = ((), (), s32[]{:S(2)}) async-start(), calls=%async_computation.15 | async-start | bytes 10027008 | tf_op jit(solution)/shard_map/reduce_scatter | solution.py:277
  335.3 352.0 %reduce-scatter.9.cloned.1.call-start = ((), (), s32[]{:S(2)}) async-start(), calls=%async_computation.14 | async-start | bytes 10027008 | tf_op jit(solution)/shard_map/reduce_scatter | solution.py:275
  348.9 344.1 %copy-start.45 = (f32[768]{0:T(1024)S(1)}, f32[768]{0:T(1024)}, u32[]{:S(2)}) copy-start(f32[768]{0:T(1024)} %get-tuple-element.17) | copy-start | bytes 9220
  348.9 344.1 %copy-start.46 = (f32[768]{0:T(1024)S(1)}, f32[768]{0:T(1024)}, u32[]{:S(2)}) copy-start(f32[768]{0:T(1024)} %get-tuple-element.48) | copy-start | bytes 9220
  348.9 344.1 %copy-start.51 = (f32[3072]{0:T(1024)S(1)}, f32[3072]{0:T(1024)}, u32[]{:S(2)}) copy-start(f32[3072]{0:T(1024)} %get-tuple-element.50) | copy-start | bytes 36868
  348.9 344.1 %copy-start.60 = (f32[768]{0:T(1024)S(1)}, f32[768]{0:T(1024)}, u32[]{:S(2)}) copy-start(f32[768]{0:T(1024)} %get-tuple-element.15) | copy-start | bytes 9220
  348.9 344.1 %copy-start.61 = (f32[768]{0:T(1024)S(1)}, f32[768]{0:T(1024)}, u32[]{:S(2)}) copy-start(f32[768]{0:T(1024)} %get-tuple-element.19) | copy-start | bytes 9220
  375.8 384.4 %all-to-all-start.1 = ((bf16[16,32,768]{2,1,0:T(8,128)(2,1)}), bf16[16,32,768]{2,1,0:T(8,128)(2,1)S(1)}, u32[]{:S(2)}, u32[]{:S(2)}) async-start(bf16[16,32,768]{2,1,0:T(8,128)(2,1)} %bitcast.189), calls=%async_computation.1 | async-start | bytes 1572864 | tf_op jit(solution)/shard_map/all_to_all | solution.py:316
  379.9 382.3 %all-reduce.22.cloned.1.call-start = ((), (), s32[]{:S(2)}) async-start(), calls=%async_computation.16 | async-start | bytes 3538944 | tf_op jit(solution)/shard_map/psum | solution.py:296
  (77 other events, 1505.1 us)
Sparse Core Ops, SparseCore 0:
  10.3 60.6 all-gather.4
  73.3 41.1 all-gather.6
  116.8 62.7 all-gather.8
  181.7 60.6 all-gather.10
  296.6 67.6 reduce-scatter.6
  368.1 89.2 reduce-scatter.4
  461.5 110.8 reduce-scatter.10
  576.5 110.8 reduce-scatter.8
  689.9 55.5 all-reduce.21
